TPU v7x, 32 devices: a whole 2x2x4 slice. The times are simulated.
32 devices in a mesh: head: 2 (over x), outer: 4 (over y, core), inner: 4 (over z).
Axes of the slice: x: 2, y: 2, z: 4, core: 2. Of those that a mesh axis runs over, the one named last changes fastest.
Arguments:
- query_mant: bfloat16 [16, 1024, 128], P('outer', ('head', 'inner')), may hold values from -40 to 40
- key_mant: bfloat16 [1, 1024, 128], P(None, ('head', 'inner')), may hold values from -10 to 10
- value_mant: bfloat16 [1, 1024, 128], P(None, ('head', 'inner')), may hold values from -4 to 4
- out_grad: bfloat16 [16, 1024, 128], P('outer', ('head', 'inner')), may hold values from -4 to 4
- query_exp: int32 [16, 8], P('outer', ('head', 'inner')), may hold values from -1 to 1
- key_exp: int32 [1, 8], P(None, ('head', 'inner')), may hold values from -1 to 1
- value_exp: int32 [1, 8], P(None, ('head', 'inner')), may hold values from -1 to 1
- block_order: int32 [8], replicated, may hold values from 0 to 7, each once
Outputs:
- attended: bfloat16 [16, 1024, 128], P('outer', ('head', 'inner'))
- query_grad: bfloat16 [16, 1024, 128], P('outer', ('head', 'inner'))
- key_grad: bfloat16 [1, 1024, 128], P(None, ('head', 'inner'))
- value_grad: bfloat16 [1, 1024, 128], P(None, ('head', 'inner'))
Inputs may be any that keep to these rules, and one draw needn't show every extreme that they name: `block_order`: every number of 0 to 7 once.
All inputs are finite; a program needn't handle non-finite values.
Results may differ from a plain program's by a relative error of at most 0.03.
Values may be sent and summed in bfloat16 or wider, within the bound.
A program may use at most 64 MiB of HBM per device.

v0:
```python
import functools
import math

import jax
import jax.numpy as jnp
from jax import lax
from jax.experimental import pallas as pl
from jax.experimental.pallas import tpu as pltpu
from jax.sharding import PartitionSpec as P

GROUP = 16
BLK = 128
MESH = pl.DeviceIdType.MESH
F32 = jnp.float32
BF16 = jnp.bfloat16


def each(count, body):
    if count <= 8:
        for index in range(count):
            body(index)
    else:
        lax.fori_loop(0, count, lambda index, carry: (body(index), carry)[1], 0)


def power(exponent):
    return jnp.where(exponent > 0, 2.0, jnp.where(exponent < 0, 0.5, 1.0)).astype(F32)


def dot_nt(left, right):
    return lax.dot_general(left, right, (((1,), (1,)), ((), ())), preferred_element_type=F32)


def dot_tn(left, right):
    return lax.dot_general(left, right, (((0,), (0,)), ((), ())), preferred_element_type=F32)


def kernel(
    sizes,
    q_hbm,
    k_hbm,
    v_hbm,
    d_hbm,
    qe_hbm,
    ke_hbm,
    ve_hbm,
    order_hbm,
    o_hbm,
    dq_hbm,
    dk_hbm,
    dv_hbm,
    kv,
    right,
    scores,
    dprob,
    left,
    part,
    half,
    half_in,
    sums,
    sums_in,
    members,
    gather_send,
    gather_recv,
    pair_send,
    pair_recv,
    half_send,
    half_recv,
    sum_send,
    sum_recv,
    out_send,
    out_recv,
    q_ref,
    k_ref,
    v_ref,
    d_ref,
    qe_ref,
    ke_ref,
    ve_ref,
    order_ref,
    o_ref,
    dq_ref,
    dk_ref,
    dv_ref,
    load_sem,
    store_sem,
):
    heads_n, inner_n, outer_n = sizes
    stores = [
        pltpu.make_async_copy(source, target, store_sem.at[at])
        for at, (source, target) in enumerate(
            ((o_ref, o_hbm), (dq_ref, dq_hbm), (dk_ref, dk_hbm), (dv_ref, dv_hbm))
        )
    ]
    loads = [
        pltpu.make_async_copy(source, target, load_sem.at[at])
        for at, (source, target) in enumerate(
            (
                (ke_hbm, ke_ref),
                (k_hbm, k_ref),
                (ve_hbm, ve_ref),
                (v_hbm, v_ref),
                (qe_hbm, qe_ref),
                (q_hbm, q_ref),
                (d_hbm, d_ref),
                (order_hbm, order_ref),
            )
        )
    ]
    heads, rows, width = q_ref.shape
    kv_count = k_ref.shape[0]
    count = heads_n * inner_n
    queries = heads * rows
    inv_root = 1.0 / math.sqrt(width)

    my_head = lax.axis_index("head")
    my_inner = lax.axis_index("inner")
    my_outer = lax.axis_index("outer")
    place = my_head * inner_n + my_inner
    core = lax.rem(my_outer, 2)
    mate = my_outer + 1 - 2 * core
    kv_index = my_outer * heads // GROUP

    offsets = [(a, b) for a in range(heads_n) for b in range(inner_n) if a or b]
    offsets.sort(key=lambda ab: min(ab[0], heads_n - ab[0]) + min(ab[1], inner_n - ab[1]))

    def ahead(off):
        return lax.rem(my_head + off[0], heads_n), lax.rem(my_inner + off[1], inner_n)

    def behind(off):
        return (
            lax.rem(my_head + heads_n - off[0], heads_n),
            lax.rem(my_inner + inner_n - off[1], inner_n),
        )

    def seq_id(pair):
        return {"head": pair[0], "inner": pair[1], "outer": my_outer}

    def outer_id(index):
        return {"head": my_head, "inner": my_inner, "outer": index}

    def index_of(pair):
        return pair[0] * inner_n + pair[1]

    barrier = pltpu.get_barrier_semaphore()
    for off in offsets:
        pl.semaphore_signal(barrier, inc=1, device_id=seq_id(ahead(off)), device_id_type=MESH)
    for step in range(1, outer_n):
        pl.semaphore_signal(
            barrier,
            inc=1,
            device_id=outer_id(lax.rem(my_outer + step, outer_n)),
            device_id_type=MESH,
        )
    for load in loads:
        load.start()
    for load in loads[:4]:
        load.wait()
    kv[0, place] = k_ref[kv_index] * power(ke_ref[kv_index, 0]).astype(BF16)
    kv[1, place] = v_ref[kv_index] * power(ve_ref[kv_index, 0]).astype(BF16)
    pl.semaphore_wait(barrier, len(offsets) + outer_n - 1)

    sends = []
    slots = {off: slot for slot, off in enumerate(offsets)}
    line = [off for off in offsets if off[0] == 0][::-1]
    across = [off for off in offsets if off[1] == 0]

    def pass_on(source, slot, device):
        return pltpu.make_async_remote_copy(
            src_ref=kv.at[core, source],
            dst_ref=kv.at[core, source],
            send_sem=gather_send.at[slot],
            recv_sem=gather_recv.at[slot],
            device_id=device,
            device_id_type=MESH,
        )

    gathers = {}
    direct = [off for off in offsets if off[0] and off[1] and min(off[1], inner_n - off[1]) == 1]
    for off in line + across + direct:
        copy = pass_on(place, slots[off], seq_id(ahead(off)))
        copy.start()
        gathers[off] = copy
        sends.append(copy)

    for load in loads[4:]:
        load.wait()
    for head in range(heads):
        right[0, head * rows : (head + 1) * rows] = q_ref[head] * power(qe_ref[head]).astype(BF16)
        right[1, head * rows : (head + 1) * rows] = d_ref[head]

    key_at = lax.broadcasted_iota(jnp.int32, (rows, queries), 0)
    row_at = lax.rem(lax.broadcasted_iota(jnp.int32, (rows, queries), 1), rows)
    lag = key_at - row_at
    own_order = order_ref[place]

    def score_block(index, top):
        reach = (own_order - order_ref[index]) * rows
        found = dot_nt(kv[0, index], right[0]) * (inv_root * math.log2(math.e))
        found = jnp.where(lag <= reach, found, -1e30)
        scores[index] = found
        dprob[index] = dot_nt(kv[1, index], right[1])
        return jnp.maximum(top, jnp.max(found.reshape(rows // 8, 8, queries), axis=0))

    top = score_block(place, jnp.full((8, queries), -1e30, F32))
    arrivals = across + line + [(a, b) for _, b in line for a, _ in across]
    waiting = None
    for off in arrivals:
        gathers[off].wait_recv()
        source = index_of(behind(off))
        if off[0] == 0:
            for step, _ in across:
                to = (step, off[1])
                if to in direct:
                    continue
                device = seq_id((lax.rem(my_head + step, heads_n), my_inner))
                copy = pass_on(source, slots[to], device)
                copy.start()
                gathers[to] = copy
                sends.append(copy)
        copy = pltpu.make_async_remote_copy(
            src_ref=kv.at[core, source],
            dst_ref=kv.at[core, source],
            send_sem=pair_send.at[slots[off]],
            recv_sem=pair_recv.at[slots[off]],
            device_id=outer_id(mate),
            device_id_type=MESH,
        )
        copy.start()
        sends.append(copy)
        if waiting is not None:
            waiting[0].wait_recv()
            top = score_block(waiting[1], top)
        waiting = (copy, source)
    if waiting is not None:
        waiting[0].wait_recv()
        top = score_block(waiting[1], top)

    best = jnp.max(top, axis=0, keepdims=True)
    half_in_f32 = jnp.zeros((8, queries), F32)

    def weigh(index, carry):
        total, cross = carry
        weight = jnp.exp2(scores[index] - best)
        scores[index] = weight
        total = total + jnp.sum(weight.reshape(rows // 8, 8, queries), axis=0)
        cross = cross + jnp.sum((weight * dprob[index]).reshape(rows // 8, 8, queries), axis=0)
        return total, cross

    carry = (half_in_f32, half_in_f32)
    if count <= 8:
        for index in range(count):
            carry = weigh(index, carry)
    else:
        carry = lax.fori_loop(0, count, weigh, carry)
    inverse = 1.0 / jnp.sum(carry[0], axis=0, keepdims=True)
    delta = jnp.sum(carry[1], axis=0, keepdims=True) * inverse

    def finish(index):
        prob = scores[index] * inverse
        left[1, index] = prob.astype(BF16)
        left[0, index] = (prob * (dprob[index] - delta)).astype(BF16)

    given = 1 - core

    def pair_copy(index):
        return pltpu.make_async_remote_copy(
            src_ref=half.at[index],
            dst_ref=half_in.at[index],
            send_sem=half_send.at[index],
            recv_sem=half_recv.at[index],
            device_id=outer_id(mate),
            device_id_type=MESH,
        )

    far = [(slot, off) for slot, off in enumerate(offsets)][::-1]
    targets = [index_of(ahead(off)) for _, off in far]
    for target in targets + [place]:
        finish(target)
        half[target] = jnp.dot(
            left[given, target], right[given], preferred_element_type=F32
        ).astype(BF16)
        pair_copy(target).start()

    sum_copies = []
    for (slot, off), target in zip(far, targets):
        kept = jnp.dot(left[core, target], right[core], preferred_element_type=F32)
        pair_copy(target).wait_recv()
        sums[slot] = (kept + half_in[target].astype(F32)).astype(BF16)
        copy = pltpu.make_async_remote_copy(
            src_ref=sums.at[slot],
            dst_ref=sums_in.at[slot],
            send_sem=sum_send.at[slot],
            recv_sem=sum_recv.at[slot],
            device_id=seq_id(ahead(off)),
            device_id_type=MESH,
        )
        copy.start()
        sum_copies.append((slot, copy))
        sends.append(copy)
    kept = jnp.dot(left[core, place], right[core], preferred_element_type=F32)
    pair_copy(place).wait_recv()
    part[...] = kept + half_in[place].astype(F32)

    flat = count * rows
    out_t = dot_tn(kv[1].reshape(flat, width), left[1].reshape(flat, queries))
    for head in range(heads):
        o_ref[head] = out_t[:, head * rows : (head + 1) * rows].T.astype(BF16)
    stores[0].start()
    dq_t = dot_tn(kv[0].reshape(flat, width), left[0].reshape(flat, queries))
    for head in range(heads):
        scale = power(qe_ref[head]) * inv_root
        dq_ref[head] = (dq_t[:, head * rows : (head + 1) * rows] * scale).T.astype(BF16)

    stores[1].start()
    total = part[...]
    for slot, copy in sum_copies:
        copy.wait_recv()
        total = total + sums_in[slot].astype(F32)
    members[my_outer] = total.astype(BF16)

    out_copies = []
    for step in range(1, outer_n):
        copy = pltpu.make_async_remote_copy(
            src_ref=members.at[my_outer],
            dst_ref=members.at[my_outer],
            send_sem=out_send.at[step - 1],
            recv_sem=out_recv.at[step - 1],
            device_id=outer_id(lax.rem(my_outer + step, outer_n)),
            device_id_type=MESH,
        )
        copy.start()
        out_copies.append(copy)
        sends.append(copy)
    for copy in out_copies:
        copy.wait_recv()
    span = outer_n // kv_count
    for group in range(kv_count):
        key_sum = jnp.zeros((rows, width), F32)
        value_sum = jnp.zeros((rows, width), F32)
        for member in range(group * span, (group + 1) * span, 2):
            key_sum = key_sum + members[member].astype(F32)
            value_sum = value_sum + members[member + 1].astype(F32)
        dk_ref[group] = (key_sum * (power(ke_ref[group, 0]) * inv_root)).astype(BF16)
        dv_ref[group] = (value_sum * power(ve_ref[group, 0])).astype(BF16)

    stores[2].start()
    stores[3].start()
    for copy in sends:
        copy.wait_send()
    each(count, lambda index: pair_copy(index).wait_send())
    for store in stores:
        store.wait()


def store_kernel(*refs):
    loads = [
        pltpu.make_async_copy(refs[at], refs[8 + at], refs[12].at[at]) for at in range(4)
    ]
    stores = [
        pltpu.make_async_copy(refs[8 + at], refs[4 + at], refs[13].at[at]) for at in range(4)
    ]
    for load in loads:
        load.start()
    for load, store in zip(loads, stores):
        load.wait()
        store.start()
    for store in stores:
        store.wait()


def on_device(
    query_mant, key_mant, value_mant, out_grad, query_exp, key_exp, value_exp, block_order, sizes
):
    heads, rows, width = query_mant.shape
    kv_count = key_mant.shape[0]
    heads_n, inner_n, outer_n = sizes
    count = heads_n * inner_n
    queries = heads * rows
    assert rows == BLK and outer_n % (2 * kv_count) == 0 and heads * outer_n == GROUP * kv_count
    dma = pltpu.SemaphoreType.DMA
    peers = max(count - 1, 1)
    hbm = pl.BlockSpec(memory_space=pltpu.HBM)
    results = pl.pallas_call(
        functools.partial(kernel, sizes),
        out_shape=(
            jax.ShapeDtypeStruct(query_mant.shape, BF16),
            jax.ShapeDtypeStruct(query_mant.shape, BF16),
            jax.ShapeDtypeStruct(key_mant.shape, BF16),
            jax.ShapeDtypeStruct(key_mant.shape, BF16),
        ),
        in_specs=[hbm] * 8,
        out_specs=(hbm,) * 4,
        scratch_shapes=[
            pltpu.VMEM((2, count, rows, width), BF16),
            pltpu.VMEM((2, queries, width), BF16),
            pltpu.VMEM((count, rows, queries), F32),
            pltpu.VMEM((count, rows, queries), F32),
            pltpu.VMEM((2, count, rows, queries), BF16),
            pltpu.VMEM((rows, width), F32),
            pltpu.VMEM((count, rows, width), BF16),
            pltpu.VMEM((count, rows, width), BF16),
            pltpu.VMEM((peers, rows, width), BF16),
            pltpu.VMEM((peers, rows, width), BF16),
            pltpu.VMEM((outer_n, rows, width), BF16),
            dma((peers,)),
            dma((peers,)),
            dma((peers,)),
            dma((peers,)),
            dma((count,)),
            dma((count,)),
            dma((peers,)),
            dma((peers,)),
            dma((outer_n,)),
            dma((outer_n,)),
            pltpu.VMEM(query_mant.shape, BF16),
            pltpu.VMEM(key_mant.shape, BF16),
            pltpu.VMEM(key_mant.shape, BF16),
            pltpu.VMEM(query_mant.shape, BF16),
            pltpu.SMEM((heads,), jnp.int32),
            pltpu.SMEM(key_exp.shape, jnp.int32),
            pltpu.SMEM(key_exp.shape, jnp.int32),
            pltpu.SMEM(block_order.shape, jnp.int32),
            pltpu.VMEM(query_mant.shape, BF16),
            pltpu.VMEM(query_mant.shape, BF16),
            pltpu.VMEM(key_mant.shape, BF16),
            pltpu.VMEM(key_mant.shape, BF16),
            dma((8,)),
            dma((4,)),
        ],
        compiler_params=pltpu.CompilerParams(
            collective_id=0, has_side_effects=True
        ),
    )(
        query_mant,
        key_mant,
        value_mant,
        out_grad,
        query_exp.reshape(-1),
        key_exp,
        value_exp,
        block_order,
    )
    return pl.pallas_call(
        store_kernel,
        out_shape=tuple(jax.ShapeDtypeStruct(found.shape, found.dtype) for found in results),
        in_specs=[hbm] * 4,
        out_specs=(hbm,) * 4,
        scratch_shapes=[pltpu.VMEM(found.shape, found.dtype) for found in results]
        + [dma((4,)), dma((4,))],
    )(*results)


def solution(mesh):
    sizes = (mesh.shape["head"], mesh.shape["inner"], mesh.shape["outer"])
    placed = (
        P("outer", ("head", "inner"), None),
        P(None, ("head", "inner"), None),
        P(None, ("head", "inner"), None),
        P("outer", ("head", "inner"), None),
        P("outer", ("head", "inner")),
        P(None, ("head", "inner")),
        P(None, ("head", "inner")),
        P(),
    )
    return jax.shard_map(
        functools.partial(on_device, sizes=sizes),
        mesh=mesh,
        in_specs=placed,
        out_specs=(
            P("outer", ("head", "inner"), None),
            P("outer", ("head", "inner"), None),
            P(None, ("head", "inner"), None),
            P(None, ("head", "inner"), None),
        ),
        check_vma=False,
    )
```

profile of v0, /device:TPU:1, one launch (start us, length us, event | category | flops | bytes accessed | tf_op | source)
XLA Modules:
  0.0 32.2 jit_solution(14292574452970328789)
XLA Ops:
  1.9 28.6 %shard_map.111 = (bf16[4,128,128]{2,1,0:T(8,128)(2,1)}, bf16[4,128,128]{2,1,0:T(8,128)(2,1)}, bf16[1,128,128]{2,1,0:T(8,128)(2,1)}, bf16[1,128,128]{2,1,0:T(8,128)(2,1)}) custom-call(bf16[4,128,128]{2,1,0:T(8,128)(2,1)} %q_hbm.1, bf16[1,128,128]{2,1,0:T(8,128)(2,1)} %k_hbm.1, bf16[1,128,128]{2,1,0:T(8,128)(2,1)} %v_hbm.1, bf16[4,128,128]{2,1,0:T(8,128)(2,1)} %d_hbm.1, ...), custom_call_target="tpu_custom_call" | custom-call | tf_op jit(solution)/shard_map/pallas_call | solution.py:384
  30.5 1.7 %shard_map.112 = (bf16[4,128,128]{2,1,0:T(8,128)(2,1)}, bf16[4,128,128]{2,1,0:T(8,128)(2,1)}, bf16[1,128,128]{2,1,0:T(8,128)(2,1)}, bf16[1,128,128]{2,1,0:T(8,128)(2,1)}) custom-call(bf16[4,128,128]{2,1,0:T(8,128)(2,1)} %get-tuple-element.8.refs_0_, bf16[4,128,128]{2,1,0:T(8,128)(2,1)} %get-tuple-element.9.refs_1_, ...), custom_call_target="tpu_custom_call" | custom-call | tf_op jit(solution)/shard_map/pallas_call | solution.py:444
where the time goes:
time: 32.7 us; the launch traced here: 32.2 us
  Pallas kernels  30.3 us (93%)
  between operations  1.93 us (6%)
    pallas_call x1, Pallas kernels, on_device(): pl.pallas_call(functools.partial(kernel, sizes), out_shape=(jax.ShapeDtyp...  28.6 us
    pallas_call x1, Pallas kernels, on_device(): pl.pallas_call(store_kernel, out_shape=tuple((jax.ShapeDtypeStruct(found....  1.71 us

commit v1 on v0

--- a/solution.py
+++ b/solution.py
@@ -45,10 +45,10 @@
     ke_hbm,
     ve_hbm,
     order_hbm,
-    o_hbm,
-    dq_hbm,
-    dk_hbm,
-    dv_hbm,
+    o_ref,
+    dq_ref,
+    dk_ref,
+    dv_ref,
     kv,
     right,
     scores,
@@ -78,20 +78,9 @@
     ke_ref,
     ve_ref,
     order_ref,
-    o_ref,
-    dq_ref,
-    dk_ref,
-    dv_ref,
     load_sem,
-    store_sem,
 ):
     heads_n, inner_n, outer_n = sizes
-    stores = [
-        pltpu.make_async_copy(source, target, store_sem.at[at])
-        for at, (source, target) in enumerate(
-            ((o_ref, o_hbm), (dq_ref, dq_hbm), (dk_ref, dk_hbm), (dv_ref, dv_hbm))
-        )
-    ]
     loads = [
         pltpu.make_async_copy(source, target, load_sem.at[at])
         for at, (source, target) in enumerate(
@@ -156,8 +145,8 @@
         load.start()
     for load in loads[:4]:
         load.wait()
-    kv[0, place] = k_ref[kv_index] * power(ke_ref[kv_index, 0]).astype(BF16)
-    kv[1, place] = v_ref[kv_index] * power(ve_ref[kv_index, 0]).astype(BF16)
+    kv[0, place] = k_ref[kv_index] * power(ke_ref[kv_index]).astype(BF16)
+    kv[1, place] = v_ref[kv_index] * power(ve_ref[kv_index]).astype(BF16)
     pl.semaphore_wait(barrier, len(offsets) + outer_n - 1)
 
     sends = []
@@ -306,13 +295,11 @@
     out_t = dot_tn(kv[1].reshape(flat, width), left[1].reshape(flat, queries))
     for head in range(heads):
         o_ref[head] = out_t[:, head * rows : (head + 1) * rows].T.astype(BF16)
-    stores[0].start()
     dq_t = dot_tn(kv[0].reshape(flat, width), left[0].reshape(flat, queries))
     for head in range(heads):
         scale = power(qe_ref[head]) * inv_root
         dq_ref[head] = (dq_t[:, head * rows : (head + 1) * rows] * scale).T.astype(BF16)
 
-    stores[1].start()
     total = part[...]
     for slot, copy in sum_copies:
         copy.wait_recv()
@@ -341,29 +328,19 @@
         for member in range(group * span, (group + 1) * span, 2):
             key_sum = key_sum + members[member].astype(F32)
             value_sum = value_sum + members[member + 1].astype(F32)
-        dk_ref[group] = (key_sum * (power(ke_ref[group, 0]) * inv_root)).astype(BF16)
-        dv_ref[group] = (value_sum * power(ve_ref[group, 0])).astype(BF16)
-
-    stores[2].start()
-    stores[3].start()
+        dk_ref[group] = (key_sum * (power(ke_ref[group]) * inv_root)).astype(BF16)
+        dv_ref[group] = (value_sum * power(ve_ref[group])).astype(BF16)
+
     for copy in sends:
         copy.wait_send()
     each(count, lambda index: pair_copy(index).wait_send())
+
+
+def store_kernel(*refs):
+    stores = [
+        pltpu.make_async_copy(refs[at], refs[4 + at], refs[8].at[at]) for at in range(4)
+    ]
     for store in stores:
-        store.wait()
-
-
-def store_kernel(*refs):
-    loads = [
-        pltpu.make_async_copy(refs[at], refs[8 + at], refs[12].at[at]) for at in range(4)
-    ]
-    stores = [
-        pltpu.make_async_copy(refs[8 + at], refs[4 + at], refs[13].at[at]) for at in range(4)
-    ]
-    for load in loads:
-        load.start()
-    for load, store in zip(loads, stores):
-        load.wait()
         store.start()
     for store in stores:
         store.wait()
@@ -381,16 +358,17 @@
     dma = pltpu.SemaphoreType.DMA
     peers = max(count - 1, 1)
     hbm = pl.BlockSpec(memory_space=pltpu.HBM)
+    vmem = pl.BlockSpec(memory_space=pltpu.VMEM)
     results = pl.pallas_call(
         functools.partial(kernel, sizes),
         out_shape=(
-            jax.ShapeDtypeStruct(query_mant.shape, BF16),
-            jax.ShapeDtypeStruct(query_mant.shape, BF16),
-            jax.ShapeDtypeStruct(key_mant.shape, BF16),
-            jax.ShapeDtypeStruct(key_mant.shape, BF16),
+            pltpu.VMEM(query_mant.shape, BF16),
+            pltpu.VMEM(query_mant.shape, BF16),
+            pltpu.VMEM(key_mant.shape, BF16),
+            pltpu.VMEM(key_mant.shape, BF16),
         ),
         in_specs=[hbm] * 8,
-        out_specs=(hbm,) * 4,
+        out_specs=(vmem,) * 4,
         scratch_shapes=[
             pltpu.VMEM((2, count, rows, width), BF16),
             pltpu.VMEM((2, queries, width), BF16),
@@ -418,15 +396,10 @@
             pltpu.VMEM(key_mant.shape, BF16),
             pltpu.VMEM(query_mant.shape, BF16),
             pltpu.SMEM((heads,), jnp.int32),
-            pltpu.SMEM(key_exp.shape, jnp.int32),
-            pltpu.SMEM(key_exp.shape, jnp.int32),
+            pltpu.SMEM((kv_count,), jnp.int32),
+            pltpu.SMEM((kv_count,), jnp.int32),
             pltpu.SMEM(block_order.shape, jnp.int32),
-            pltpu.VMEM(query_mant.shape, BF16),
-            pltpu.VMEM(query_mant.shape, BF16),
-            pltpu.VMEM(key_mant.shape, BF16),
-            pltpu.VMEM(key_mant.shape, BF16),
             dma((8,)),
-            dma((4,)),
         ],
         compiler_params=pltpu.CompilerParams(
             collective_id=0, has_side_effects=True
@@ -437,18 +410,17 @@
         value_mant,
         out_grad,
         query_exp.reshape(-1),
-        key_exp,
-        value_exp,
+        key_exp.reshape(-1),
+        value_exp.reshape(-1),
         block_order,
     )
     return pl.pallas_call(
         store_kernel,
         out_shape=tuple(jax.ShapeDtypeStruct(found.shape, found.dtype) for found in results),
-        in_specs=[hbm] * 4,
+        in_specs=[vmem] * 4,
         out_specs=(hbm,) * 4,
-        scratch_shapes=[pltpu.VMEM(found.shape, found.dtype) for found in results]
-        + [dma((4,)), dma((4,))],
-    )(*results)
+        scratch_shapes=[dma((4,))],
+    )(*(pltpu.with_memory_space_constraint(found, pltpu.VMEM) for found in results))
 
 
 def solution(mesh):

time: 32.7 us -> 31.1 us (0.951)
  Pallas kernels: 30.3 us -> 28.7 us
    pallas_call x1, Pallas kernels: 1.71 us -> 0.75 us  [on_device(): pl.pallas_call(store_kernel, out_shape=tuple((jax.ShapeDtypeStruct(found....]
    pallas_call x1, Pallas kernels: 28.6 us -> 28 us  [on_device(): pl.pallas_call(functools.partial(kernel, sizes), out_shape=(pltpu.VMEM(qu...]
where the time goes in v1:
time: 31.1 us; the launch traced here: 30.7 us
  Pallas kernels  28.7 us (92%)
  between operations  1.93 us (6%)
    pallas_call x1, Pallas kernels, on_device(): pl.pallas_call(functools.partial(kernel, sizes), out_shape=(pltpu.VMEM(qu...  28 us
    pallas_call x1, Pallas kernels, on_device(): pl.pallas_call(store_kernel, out_shape=tuple((jax.ShapeDtypeStruct(found....  0.75 us

profile of v1, /device:TPU:1, one launch (start us, length us, event | category | flops | bytes accessed | tf_op | source)
XLA Modules:
  0.0 30.7 jit_solution(13194207793030472204)
XLA Ops:
  1.9 28.0 %shard_map.111 = (bf16[4,128,128]{2,1,0:T(8,128)(2,1)S(1)}, bf16[4,128,128]{2,1,0:T(8,128)(2,1)S(1)}, bf16[1,128,128]{2,1,0:T(8,128)(2,1)S(1)}, bf16[1,128,128]{2,1,0:T(8,128)(2,1)S(1)}) custom-call(bf16[4,128,128]{2,1,0:T(8,128)(2,1)} %q_hbm.1, bf16[1,128,128]{2,1,0:T(8,128)(2,1)} %k_hbm.1, bf16[1,128,128]{2,1,0:T(8,128)(2,1)} %v_hbm.1, ...), custom_call_target="tpu_custom_call" | custom-call | tf_op jit(solution)/shard_map/pallas_call | solution.py:362
  29.9 0.7 %shard_map.112 = (bf16[4,128,128]{2,1,0:T(8,128)(2,1)}, bf16[4,128,128]{2,1,0:T(8,128)(2,1)}, bf16[1,128,128]{2,1,0:T(8,128)(2,1)}, bf16[1,128,128]{2,1,0:T(8,128)(2,1)}) custom-call(bf16[4,128,128]{2,1,0:T(8,128)(2,1)S(1)} %get-tuple-element.8.refs_0_, bf16[4,128,128]{2,1,0:T(8,128)(2,1)S(1)} %get-tuple-element.9.refs_1_, ...), custom_call_target="tpu_custom_call" | custom-call | tf_op jit(solution)/shard_map/pallas_call | solution.py:417
